TPU v7x, 64 devices: a 2x2x8 block of a 4x4x8 slice. The times are simulated.
64 devices in a mesh: dp: 8 (over x, y, core), tp: 8 (over z).
Axes of the slice: x: 2, y: 2, z: 8, core: 2. Of those that a mesh axis runs over, the one named last changes fastest.
The devices are a block of a 4x4x8 slice.
Arguments:
- x: bfloat16 [16384, 4096], P('dp'), parts along dimension 0
- w_gate: bfloat16 [4096, 16384], P(None, 'tp')
- w_up: bfloat16 [4096, 16384], P(None, 'tp')
- w_down: bfloat16 [16384, 4096], P('tp')
Outputs:
- output: bfloat16 [16384, 4096], P('dp'), parts along dimension 0
There are 8 independent parts. A program takes and returns all parts, laid end to end along the dimension named above; an argument that names none is the same for every part.
All inputs are finite; a program needn't handle non-finite values.
Results may differ from a plain program's by a relative error of at most 0.016.
Values are sent between devices in bfloat16 or wider.
A program may use at most 768 MiB of HBM per device.

v0:
```python
import jax
import jax.numpy as jnp
from jax import lax
from jax.sharding import PartitionSpec as P


def solution(mesh):
    def step(x, w_gate, w_up, w_down):
        gate = jnp.dot(x, w_gate, preferred_element_type=jnp.float32)
        up = jnp.dot(x, w_up, preferred_element_type=jnp.float32)
        hidden = (jax.nn.silu(gate) * up).astype(jnp.bfloat16)
        term = jnp.dot(hidden, w_down, preferred_element_type=jnp.float32).astype(jnp.bfloat16)
        return lax.psum(term, "tp")

    return jax.shard_map(
        step,
        mesh=mesh,
        in_specs=(P("dp", None), P(None, "tp"), P(None, "tp"), P("tp", None)),
        out_specs=P("dp", None),
        check_vma=False,
    )
```

profile of v0, /device:TPU:21, one launch (start us, length us, event | category | flops | bytes accessed | tf_op | source)
XLA Modules:
  0.0 501.3 jit_solution(7078354643899704784)
XLA Ops:
  6.5 0.0 all-reduce.2.cloned.1.call-start
  6.6 43.0 %fusion = f32[2048,2048]{1,0:T(8,128)} fusion(bf16[2048,4096]{1,0:T(8,128)(2,1)} %param.4, bf16[4096,2048]{1,0:T(8,128)(2,1)} %param.5), kind=kOutput, calls=%fused_computation.2 | convolution fusion | flops 34359738368 | bytes 50331648 | tf_op jit(solution)/shard_map/dot_general | solution.py:9
  49.6 46.7 %multiply_convert_fusion = bf16[2048,2048]{1,0:T(8,128)(2,1)S(1)} fusion(f32[2048,2048]{1,0:T(8,128)} %fusion, bf16[2048,4096]{1,0:T(8,128)(2,1)} %param.4, bf16[4096,2048]{1,0:T(8,128)(2,1)} %param.6), kind=kOutput, calls=%fused_computation | convolution fusion | flops 34384904192 | bytes 58720256 | tf_op jit(solution)/shard_map/dot_general | solution.py:10
  96.3 41.0 %convolution_convert_fusion = bf16[2048,4096]{1,0:T(8,128)(2,1)} fusion(bf16[2048,2048]{1,0:T(8,128)(2,1)S(1)} %multiply_convert_fusion, bf16[2048,4096]{1,0:T(8,128)(2,1)} %param.7), kind=kOutput, calls=%fused_computation.1 | convolution fusion | flops 34368126976 | bytes 41943040 | tf_op jit(solution)/shard_map/dot_general | solution.py:12
  137.3 0.1 all-reduce.2.cloned.1.call-update
  137.3 343.0 %all-reduce.2.cloned.1.call-done = bf16[2048,4096]{1,0:T(8,128)(2,1)} async-done(((bf16[2048,4096]{1,0:T(8,128)(2,1)}), bf16[2048,4096]{1,0:T(8,128)(2,1)}) %all-reduce.2.cloned.1.call-update) | async-done | bytes 16777232 | tf_op jit(solution)/shard_map/psum | solution.py:13
  480.4 14.1 %copy.6 = bf16[2048,4096]{1,0:T(8,128)(2,1)} copy(bf16[2048,4096]{1,0:T(8,128)(2,1)} %all-reduce.2.cloned.1.call-done) | data formatting | bytes 33554432
Async XLA Ops:
  6.5 473.8 %all-reduce.2.cloned.1.call-start = ((), (), s32[]{:S(2)}) async-start(), calls=%async_computation | async-start | bytes 33554432 | tf_op jit(solution)/shard_map/psum | solution.py:13
Sparse Core Ops, SparseCore 0:
  137.5 342.8 all-reduce.1
where the time goes:
time: 501 us
  waiting for transfers between devices  343 us (68%)
  matrix products  131 us (26%)
  local copies, waits for them, and re-layouts  14.1 us (3%)
  between operations  13.4 us (3%)
    psum x1, waiting for transfers between devices, step(): return lax.psum(term, 'tp')  343 us
    dot_general x1, matrix products, step(): up = jnp.dot(x, w_up, preferred_element_type=jnp.float32)  46.7 us
    dot_general x1, matrix products, step(): gate = jnp.dot(x, w_gate, preferred_element_type=jnp.float32)  43 us
    dot_general x1, matrix products, step(): jnp.dot(hidden, w_down, preferred_element_type=jnp.float32)  41 us
    unnamed x1, local copies, waits for them, and re-layouts  14.1 us
  transfers between devices with their start and end apart: 1, of which 1 were waited for; matrix products, arithmetic and copies ran while one was open for 0% of the time, Pallas kernels for 0%

commit v1 on v0

v1 whole, which is shorter than its diff:
```python
import functools

import jax
import jax.numpy as jnp
from jax import lax
from jax.experimental import pallas as pl
from jax.experimental.pallas import tpu as pltpu
from jax.sharding import PartitionSpec as P

MESH = pl.DeviceIdType.MESH
FB = 256
DB = 512


def ring_kernel(
    n, x, wg, wu, wd, y, wgv, wuv, wdv, xv, hv, tv, land, out,
    w_sem, d_sem, x_sem, send_rs, recv_rs, send_ag, recv_ag, y_sem,
):
    me = lax.axis_index("tp")
    rows, cols = x.shape
    hidden = wg.shape[1]
    half = rows // 2
    rb = half // n
    nj, nc = hidden // FB, cols // DB
    peers = (lax.rem(me + 1, n), lax.rem(me + n - 1, n))

    def block_rows(d, s):
        b = lax.rem(me + 2 * n - s, n) if d == 0 else lax.rem(me + s, n)
        return pl.ds(pl.multiple_of(d * half + b * rb, rb), rb)

    def columns(i, size):
        return pl.ds(pl.multiple_of(i * size, size), size)

    def load_w(j):
        c = columns(j, FB)
        return (
            pltpu.make_async_copy(wg.at[:, c], wgv.at[:, c], w_sem.at[0, j]),
            pltpu.make_async_copy(wu.at[:, c], wuv.at[:, c], w_sem.at[1, j]),
        )

    def load_d(c):
        k = columns(c, DB)
        return pltpu.make_async_copy(wd.at[:, k], wdv.at[:, k], d_sem.at[c])

    def load_x(d, s):
        return pltpu.make_async_copy(
            x.at[block_rows(d, s), :], xv.at[pl.ds(d * rb, rb), :], x_sem.at[d]
        )

    def remote(src, dst, ssem, rsem, d):
        return pltpu.make_async_remote_copy(
            src_ref=src, dst_ref=dst, send_sem=ssem, recv_sem=rsem,
            device_id={"tp": peers[d]}, device_id_type=MESH,
        )

    def hop(d, s, c):
        now, later = lax.rem(s, 2), lax.rem(s + 1, 2)
        return remote(
            out.at[d, now, c], land.at[d, later, c],
            send_rs.at[d, now, c], recv_rs.at[d, later, c], d,
        )

    def gather_hop(d, t, c):
        there = y.at[block_rows(d, n - 1 + t), columns(c, DB)]
        return remote(there, there, send_ag.at[d, t, c], recv_ag.at[d, t, c], d)

    def first_gather_hop(d, c):
        there = y.at[block_rows(d, n - 1), columns(c, DB)]
        return remote(
            out.at[d, (n - 1) % 2, c], there, send_ag.at[d, 0, c], recv_ag.at[d, 0, c], d
        )

    def keep(d, c):
        return pltpu.make_async_copy(
            out.at[d, (n - 1) % 2, c],
            y.at[block_rows(d, n - 1), columns(c, DB)],
            y_sem.at[d, c],
        )

    for d in range(2):
        load_x(d, 0).start()
    for j in range(2):
        for copy in load_w(j):
            copy.start()

    barrier = pltpu.get_barrier_semaphore()
    for peer in peers:
        pl.semaphore_signal(barrier, inc=1, device_id={"tp": peer}, device_id_type=MESH)
    pl.semaphore_wait(barrier, 2)

    def ring_step(s, _):
        for d in range(2):
            load_x(d, s).wait()

        def gate_up(j, _):
            @pl.when(s == 0)
            def _():
                for copy in load_w(j):
                    copy.wait()

                @pl.when(j + 2 < nj)
                def _():
                    for copy in load_w(j + 2):
                        copy.start()

                @pl.when(j + 2 >= nj)
                def _():
                    for i in range(nc // 2):
                        load_d((j + 2 - nj) * (nc // 2) + i).start()

            k = columns(j, FB)
            gate = jnp.dot(xv[...], wgv[:, k], preferred_element_type=jnp.float32)
            up = jnp.dot(xv[...], wuv[:, k], preferred_element_type=jnp.float32)
            hv[:, k] = (jax.nn.silu(gate) * up).astype(jnp.bfloat16)
            return 0

        lax.fori_loop(0, nj, gate_up, 0)

        @pl.when(s < n - 1)
        def _():
            for d in range(2):
                load_x(d, s + 1).start()

        now = lax.rem(s, 2)

        def down(c, _):
            @pl.when(s == 0)
            def _():
                load_d(c).wait()

            tv[...] = jnp.dot(hv[...], wdv[:, columns(c, DB)], preferred_element_type=jnp.float32)

            @pl.when(s >= 2)
            def _():
                for d in range(2):
                    hop(d, s - 2, c).wait_send()

            @pl.when(s == 0)
            def _():
                for d in range(2):
                    out[d, now, c] = tv[d * rb:(d + 1) * rb, :].astype(jnp.bfloat16)

            @pl.when(s > 0)
            def _():
                for d in range(2):
                    hop(d, s - 1, c).wait_recv()
                for d in range(2):
                    total = land[d, now, c].astype(jnp.float32) + tv[d * rb:(d + 1) * rb, :]
                    out[d, now, c] = total.astype(jnp.bfloat16)

            @pl.when(s < n - 1)
            def _():
                for d in range(2):
                    hop(d, s, c).start()

            @pl.when(s == n - 1)
            def _():
                for d in range(2):
                    first_gather_hop(d, c).start()
                for d in range(2):
                    keep(d, c).start()

            return 0

        lax.fori_loop(0, nc, down, 0)
        return 0

    lax.fori_loop(0, n, ring_step, 0)

    def gather_step(t, _):
        def piece(c, _):
            for d in range(2):
                gather_hop(d, t, c).wait_recv()

                @pl.when(t < n - 2)
                def _():
                    gather_hop(d, t + 1, c).start()

            return 0

        return lax.fori_loop(0, nc, piece, 0)

    lax.fori_loop(0, n - 1, gather_step, 0)

    def finish(c, _):
        for d in range(2):
            hop(d, n - 2, c).wait_send()
            first_gather_hop(d, c).wait_send()
            keep(d, c).wait()

            def sent(t, _):
                gather_hop(d, t, c).wait_send()
                return 0

            lax.fori_loop(1, n - 1, sent, 0)
        return 0

    lax.fori_loop(0, nc, finish, 0)


def solution(mesh):
    n = mesh.shape["tp"]

    def step(x, w_gate, w_up, w_down):
        rows, cols = x.shape
        hidden = w_gate.shape[1]
        rb = rows // 2 // n
        nj, nc = hidden // FB, cols // DB
        dma = pltpu.SemaphoreType.DMA
        return pl.pallas_call(
            functools.partial(ring_kernel, n),
            name="mlp_ring",
            out_shape=jax.ShapeDtypeStruct((rows, cols), jnp.bfloat16),
            in_specs=[pl.BlockSpec(memory_space=pl.ANY)] * 4,
            out_specs=pl.BlockSpec(memory_space=pl.ANY),
            scratch_shapes=[
                pltpu.VMEM(w_gate.shape, jnp.bfloat16),
                pltpu.VMEM(w_up.shape, jnp.bfloat16),
                pltpu.VMEM(w_down.shape, jnp.bfloat16),
                pltpu.VMEM((2 * rb, cols), jnp.bfloat16),
                pltpu.VMEM((2 * rb, hidden), jnp.bfloat16),
                pltpu.VMEM((2 * rb, DB), jnp.float32),
                pltpu.VMEM((2, 2, nc, rb, DB), jnp.bfloat16),
                pltpu.VMEM((2, 2, nc, rb, DB), jnp.bfloat16),
                dma((2, nj)),
                dma((nc,)),
                dma((2,)),
                dma((2, 2, nc)),
                dma((2, 2, nc)),
                dma((2, n - 1, nc)),
                dma((2, n - 1, nc)),
                dma((2, nc)),
            ],
            compiler_params=pltpu.CompilerParams(
                collective_id=0, has_side_effects=True, vmem_limit_bytes=67043328
            ),
        )(x, w_gate, w_up, w_down)

    return jax.shard_map(
        step,
        mesh=mesh,
        in_specs=(P("dp", None), P(None, "tp"), P(None, "tp"), P("tp", None)),
        out_specs=P("dp", None),
        check_vma=False,
    )
```

time: 501 us -> 356 us (0.71)
  waiting for transfers between devices: 343 us -> 0 us
  Pallas kernels: 0 us -> 341 us
  matrix products: 131 us -> 0 us
  between operations: 13.4 us -> 0.01 us
    psum x1 -> x0, waiting for transfers between devices: 343 us -> none  [step(): return lax.psum(term, 'tp')]
    pallas_call x0 -> x1, Pallas kernels: none -> 341 us  [step(): pl.pallas_call(functools.partial(ring_kernel, n), name='mlp_ring', out_sh...]
    dot_general x3 -> x0, matrix products: 131 us -> none  [the longest x1 46.7 us: step(): up = jnp.dot(x, w_up, preferred_element_type=jnp.float32)]
  transfers between devices with their start and end apart: 1 -> 0, of which waited for: 1 -> 0; matrix products, arithmetic and copies ran while one was open for 0% -> 0% of each run, Pallas kernels for 0% -> 0%
where the time goes in v1:
time: 356 us; the launch traced here: 355 us
  Pallas kernels  341 us (96%)
  local copies, waits for them, and re-layouts  14.1 us (4%)
    pallas_call x1, Pallas kernels, step(): pl.pallas_call(functools.partial(ring_kernel, n), name='mlp_ring', out_sh...  341 us
    unnamed x1, local copies, waits for them, and re-layouts  14.1 us

profile of v1, /device:TPU:21, one launch (start us, length us, event | category | flops | bytes accessed | tf_op | source)
XLA Modules:
  0.0 355.4 jit_solution(12104968214519525913)
XLA Ops:
  0.0 341.3 %mlp_ring.1 = bf16[2048,4096]{1,0:T(8,128)(2,1)} custom-call(bf16[2048,4096]{1,0:T(8,128)(2,1)} %x.1, bf16[4096,2048]{1,0:T(8,128)(2,1)} %wg.1, bf16[4096,2048]{1,0:T(8,128)(2,1)} %wu.1, bf16[2048,4096]{1,0:T(8,128)(2,1)} %wd.1), custom_call_target="tpu_custom_call" | custom-call | tf_op jit(solution)/shard_map/mlp_ring/pallas_call | solution.py:210
  341.3 14.1 %copy.6 = bf16[2048,4096]{1,0:T(8,128)(2,1)} copy(bf16[2048,4096]{1,0:T(8,128)(2,1)} %mlp_ring.1) | data formatting | bytes 33554432

commit v2 on v1

v2 whole, which is shorter than its diff:
```python
import functools

import jax
import jax.numpy as jnp
from jax import lax
from jax.experimental import pallas as pl
from jax.experimental.pallas import tpu as pltpu
from jax.sharding import PartitionSpec as P

MESH = pl.DeviceIdType.MESH
FB = 256
DB = 1024
AHEAD = 2


def ring_kernel(
    n, x, wg, wu, wd, held, wuv, wdv, xv, hv, tv, land, out,
    w_sem, d_sem, x_sem, send_rs, recv_rs, send_ag, recv_ag, free_sem,
):
    me = lax.axis_index("tp")
    rows, cols = x.shape
    hidden = wg.shape[1]
    half = rows // 2
    rb = half // n
    nj, nc, strips = hidden // FB, cols // DB, DB // FB
    peers = (lax.rem(me + 1, n), lax.rem(me + n - 1, n))

    def block(d, s):
        return lax.rem(me + 2 * n - s, n) if d == 0 else lax.rem(me + s, n)

    def span(i, size):
        return pl.ds(pl.multiple_of(i * size, size), size)

    def load_w(j):
        k = span(j, FB)
        return (
            pltpu.make_async_copy(wg.at[:, k], held.at[span(j, cols), :], w_sem.at[0, j]),
            pltpu.make_async_copy(wu.at[:, k], wuv.at[:, k], w_sem.at[1, j]),
        )

    def load_d(c):
        k = span(c, DB)
        return pltpu.make_async_copy(wd.at[:, k], wdv.at[:, k], d_sem.at[c])

    def load_x(d, s):
        start = pl.multiple_of(d * half + block(d, s) * rb, rb)
        return pltpu.make_async_copy(
            x.at[pl.ds(start, rb), :], xv.at[pl.ds(d * rb, rb), :], x_sem.at[d]
        )

    def remote(src, dst, ssem, rsem, d):
        return pltpu.make_async_remote_copy(
            src_ref=src, dst_ref=dst, send_sem=ssem, recv_sem=rsem,
            device_id={"tp": peers[d]}, device_id_type=MESH,
        )

    def hop(d, s, c):
        now, later = lax.rem(s, 2), lax.rem(s + 1, 2)
        return remote(
            out.at[d, now, c], land.at[d, later, c],
            send_rs.at[d, now, c], recv_rs.at[d, later, c], d,
        )

    def piece_start(d, s, c):
        return ((d * n + block(d, s)) * nc + c) * (strips * rb)

    def gather_hop(d, t, c):
        p = held.at[pl.ds(pl.multiple_of(piece_start(d, n - 1 + t, c), rb), strips * rb), :]
        return remote(p, p, send_ag.at[d, t, c], recv_ag.at[d, t, c], d)

    for d in range(2):
        load_x(d, 0).start()
    for j in range(AHEAD):
        for copy in load_w(j):
            copy.start()

    barrier = pltpu.get_barrier_semaphore()
    for peer in peers:
        pl.semaphore_signal(barrier, inc=1, device_id={"tp": peer}, device_id_type=MESH)
    pl.semaphore_wait(barrier, 2)

    def ring_step(s, _):
        for d in range(2):
            load_x(d, s).wait()

        def gate_up(j, _):
            @pl.when(s == 0)
            def _():
                for copy in load_w(j):
                    copy.wait()

                @pl.when(j + AHEAD < nj)
                def _():
                    for copy in load_w(j + AHEAD):
                        copy.start()

                @pl.when(j + AHEAD >= nj)
                def _():
                    for i in range(nc // AHEAD):
                        load_d((j + AHEAD - nj) * (nc // AHEAD) + i).start()

            gate = jnp.dot(xv[...], held[span(j, cols), :], preferred_element_type=jnp.float32)
            up = jnp.dot(xv[...], wuv[:, span(j, FB)], preferred_element_type=jnp.float32)
            hv[:, span(j, FB)] = (jax.nn.silu(gate) * up).astype(jnp.bfloat16)
            return 0

        lax.fori_loop(0, nj, gate_up, 0)

        @pl.when(s < n - 1)
        def _():
            for d in range(2):
                load_x(d, s + 1).start()

        @pl.when(s == n - 1)
        def _():
            for peer in peers:
                pl.semaphore_signal(free_sem, inc=1, device_id={"tp": peer}, device_id_type=MESH)
            pl.semaphore_wait(free_sem, 2)

        now = lax.rem(s, 2)

        def down(c, _):
            @pl.when(s == 0)
            def _():
                load_d(c).wait()

            tv[...] = jnp.dot(hv[...], wdv[:, span(c, DB)], preferred_element_type=jnp.float32)

            def term(d, i):
                return tv[d * rb:(d + 1) * rb, i * FB:(i + 1) * FB]

            def arrived(d, i):
                return land[d, now, c, i * rb:(i + 1) * rb, :].astype(jnp.float32)

            @pl.when((s >= 2) & (s < n - 1))
            def _():
                for d in range(2):
                    hop(d, s - 2, c).wait_send()

            @pl.when(s > 0)
            def _():
                for d in range(2):
                    hop(d, s - 1, c).wait_recv()

            @pl.when(s == 0)
            def _():
                for d in range(2):
                    for i in range(strips):
                        out[d, now, c, i * rb:(i + 1) * rb, :] = term(d, i).astype(jnp.bfloat16)

            @pl.when((s > 0) & (s < n - 1))
            def _():
                for d in range(2):
                    for i in range(strips):
                        total = arrived(d, i) + term(d, i)
                        out[d, now, c, i * rb:(i + 1) * rb, :] = total.astype(jnp.bfloat16)

            @pl.when(s < n - 1)
            def _():
                for d in range(2):
                    hop(d, s, c).start()

            @pl.when(s == n - 1)
            def _():
                for d in range(2):
                    for i in range(strips):
                        start = pl.multiple_of(piece_start(d, n - 1, c) + i * rb, rb)
                        total = arrived(d, i) + term(d, i)
                        held[pl.ds(start, rb), :] = total.astype(jnp.bfloat16)
                for d in range(2):
                    gather_hop(d, 0, c).start()

            return 0

        lax.fori_loop(0, nc, down, 0)
        return 0

    lax.fori_loop(0, n, ring_step, 0)

    def gather_step(t, _):
        def piece(c, _):
            for d in range(2):
                gather_hop(d, t, c).wait_recv()

                @pl.when(t < n - 2)
                def _():
                    gather_hop(d, t + 1, c).start()

            return 0

        return lax.fori_loop(0, nc, piece, 0)

    lax.fori_loop(0, n - 1, gather_step, 0)

    def finish(c, _):
        for d in range(2):
            hop(d, n - 3, c).wait_send()
            hop(d, n - 2, c).wait_send()

            def sent(t, _):
                gather_hop(d, t, c).wait_send()
                return 0

            lax.fori_loop(0, n - 1, sent, 0)
        return 0

    lax.fori_loop(0, nc, finish, 0)


def place_kernel(n, held, y, sem):
    rows, cols = y.shape
    rb = rows // 2 // n
    nk = cols // FB

    def copy(i):
        r, k = lax.div(i, nk), lax.rem(i, nk)
        return pltpu.make_async_copy(
            held.at[pl.ds(pl.multiple_of(i * rb, rb), rb), :],
            y.at[pl.ds(pl.multiple_of(r * rb, rb), rb), pl.ds(pl.multiple_of(k * FB, FB), FB)],
            sem.at[i],
        )

    def start(i, _):
        copy(i).start()
        return 0

    def wait(i, _):
        copy(i).wait()
        return 0

    lax.fori_loop(0, 2 * n * nk, start, 0)
    lax.fori_loop(0, 2 * n * nk, wait, 0)


def solution(mesh):
    n = mesh.shape["tp"]

    def step(x, w_gate, w_up, w_down):
        rows, cols = x.shape
        hidden = w_gate.shape[1]
        rb = rows // 2 // n
        nj, nc = hidden // FB, cols // DB
        dma = pltpu.SemaphoreType.DMA
        bf16 = jnp.bfloat16
        held = pl.pallas_call(
            functools.partial(ring_kernel, n),
            name="mlp_ring",
            out_shape=pltpu.VMEM((max(rows, hidden) * cols // FB, FB), bf16),
            in_specs=[pl.BlockSpec(memory_space=pl.ANY)] * 4,
            out_specs=pl.BlockSpec(memory_space=pltpu.VMEM),
            scratch_shapes=[
                pltpu.VMEM(w_up.shape, bf16),
                pltpu.VMEM(w_down.shape, bf16),
                pltpu.VMEM((2 * rb, cols), bf16),
                pltpu.VMEM((2 * rb, hidden), bf16),
                pltpu.VMEM((2 * rb, DB), jnp.float32),
                pltpu.VMEM((2, 2, nc, rb * DB // FB, FB), bf16),
                pltpu.VMEM((2, 2, nc, rb * DB // FB, FB), bf16),
                dma((2, nj)),
                dma((nc,)),
                dma((2,)),
                dma((2, 2, nc)),
                dma((2, 2, nc)),
                dma((2, n - 1, nc)),
                dma((2, n - 1, nc)),
                pltpu.SemaphoreType.REGULAR,
            ],
            compiler_params=pltpu.CompilerParams(
                collective_id=0, has_side_effects=True, vmem_limit_bytes=46 * 2**20
            ),
        )(x, w_gate, w_up, w_down)
        return pl.pallas_call(
            functools.partial(place_kernel, n),
            name="place",
            out_shape=jax.ShapeDtypeStruct((rows, cols), bf16),
            in_specs=[pl.BlockSpec(memory_space=pltpu.VMEM)],
            out_specs=pl.BlockSpec(memory_space=pl.ANY),
            scratch_shapes=[dma((2 * n * cols // FB,))],
            compiler_params=pltpu.CompilerParams(vmem_limit_bytes=2**20),
        )(held)

    return jax.shard_map(
        step,
        mesh=mesh,
        in_specs=(P("dp", None), P(None, "tp"), P(None, "tp"), P("tp", None)),
        out_specs=P("dp", None),
        check_vma=False,
    )
```

time: 356 us -> 349 us (0.980)
  local copies, waits for them, and re-layouts: 14.1 us -> 0 us
  Pallas kernels: 341 us -> 349 us
    unnamed x1 -> x0, local copies, waits for them, and re-layouts: 14.1 us -> none
    pallas_call x0 -> x1, Pallas kernels: none -> 7.99 us  [step(): pl.pallas_call(functools.partial(place_kernel, n), name='place', out_shap...]
where the time goes in v2:
time: 349 us
  Pallas kernels  349 us (100%)
    pallas_call x1, Pallas kernels, step(): pl.pallas_call(functools.partial(ring_kernel, n), name='mlp_ring', out_sh...  341 us
    pallas_call x1, Pallas kernels, step(): pl.pallas_call(functools.partial(place_kernel, n), name='place', out_shap...  7.99 us

profile of v2, /device:TPU:21, one launch (start us, length us, event | category | flops | bytes accessed | tf_op | source)
XLA Modules:
  0.0 348.5 jit_solution(7284571742179441537)
XLA Ops:
  0.0 340.5 %mlp_ring.1.held = bf16[32768,256]{1,0:T(8,128)(2,1)S(1)} custom-call(bf16[2048,4096]{1,0:T(8,128)(2,1)} %x.1, bf16[4096,2048]{1,0:T(8,128)(2,1)} %wg.1, bf16[4096,2048]{1,0:T(8,128)(2,1)} %wu.1, bf16[2048,4096]{1,0:T(8,128)(2,1)} %wd.1), custom_call_target="tpu_custom_call" | custom-call | tf_op jit(solution)/shard_map/mlp_ring/pallas_call | solution.py:245
  340.5 8.0 %place.1 = bf16[2048,4096]{1,0:T(8,128)(2,1)} custom-call(bf16[32768,256]{1,0:T(8,128)(2,1)S(1)} %mlp_ring.1.held), custom_call_target="tpu_custom_call" | custom-call | tf_op jit(solution)/shard_map/place/pallas_call | solution.py:272

commit v3 on v1

--- a/solution.py
+++ b/solution.py
@@ -9,11 +9,11 @@
 
 MESH = pl.DeviceIdType.MESH
 FB = 256
-DB = 512
+DB = 1024
 
 
 def ring_kernel(
-    n, x, wg, wu, wd, y, wgv, wuv, wdv, xv, hv, tv, land, out,
+    n, x, wg, wu, wd, y, right, left, wgv, wuv, wdv, xv, hv, tv, land, out,
     w_sem, d_sem, x_sem, send_rs, recv_rs, send_ag, recv_ag, y_sem,
 ):
     me = lax.axis_index("tp")
@@ -70,6 +70,12 @@
             out.at[d, (n - 1) % 2, c], there, send_ag.at[d, 0, c], recv_ag.at[d, 0, c], d
         )
 
+    def side_hop(d, c):
+        t = n - 3
+        here = y.at[block_rows(d, n - 1 + t), columns(c, DB)]
+        there = (right, left)[d].at[:, columns(c, DB)]
+        return remote(here, there, send_ag.at[d, t, c], recv_ag.at[d, t, c], d)
+
     def keep(d, c):
         return pltpu.make_async_copy(
             out.at[d, (n - 1) % 2, c],
@@ -171,16 +177,20 @@
         def piece(c, _):
             for d in range(2):
                 gather_hop(d, t, c).wait_recv()
-
-                @pl.when(t < n - 2)
-                def _():
-                    gather_hop(d, t + 1, c).start()
-
+                gather_hop(d, t + 1, c).start()
             return 0
 
         return lax.fori_loop(0, nc, piece, 0)
 
-    lax.fori_loop(0, n - 1, gather_step, 0)
+    lax.fori_loop(0, n - 4, gather_step, 0)
+
+    def aside(c, _):
+        for d in range(2):
+            gather_hop(d, n - 4, c).wait_recv()
+            side_hop(d, c).start()
+        return 0
+
+    lax.fori_loop(0, nc, aside, 0)
 
     def finish(c, _):
         for d in range(2):
@@ -192,10 +202,72 @@
                 gather_hop(d, t, c).wait_send()
                 return 0
 
-            lax.fori_loop(1, n - 1, sent, 0)
+            lax.fori_loop(1, n - 3, sent, 0)
         return 0
 
     lax.fori_loop(0, nc, finish, 0)
+
+    def arrive(c, _):
+        for d in range(2):
+            side_hop(d, c).wait()
+        return 0
+
+    lax.fori_loop(0, nc, arrive, 0)
+
+
+def place_kernel(n, ring, right, left, y, buf, in_sem, out_sem):
+    me = lax.axis_index("tp")
+    half = y.shape[0] // 2
+    rb = half // n
+
+    def at(d, s):
+        b = lax.rem(me + 3 * n - s, n) if d == 0 else lax.rem(me + s, n)
+        return pl.ds(pl.multiple_of(d * half + b * rb, rb), rb)
+
+    def copy_in(d, i):
+        return pltpu.make_async_copy(ring.at[at(d, n - 1 + i), :], buf.at[d, i], in_sem.at[d, i])
+
+    def copy_out(d, i):
+        return pltpu.make_async_copy(buf.at[d, i], y.at[at(d, n - 1 + i), :], out_sem.at[d, i])
+
+    def copy_side(d):
+        return pltpu.make_async_copy(
+            (right, left)[d], y.at[at(d, 2 * n - 3), :], out_sem.at[d, n - 2]
+        )
+
+    for i in range(n - 2):
+        for d in range(2):
+            copy_in(d, i).start()
+    for d in range(2):
+        copy_side(d).start()
+    for i in range(n - 2):
+        for d in range(2):
+            copy_in(d, i).wait()
+            copy_out(d, i).start()
+    for d in range(2):
+        for i in range(n - 2):
+            copy_out(d, i).wait()
+        copy_side(d).wait()
+
+
+def place_last_kernel(n, _, right, left, y, sem):
+    me = lax.axis_index("tp")
+    half = y.shape[0] // 2
+    rb = half // n
+    copies = []
+    for d in range(2):
+        b = lax.rem(me + n + 2, n) if d == 0 else lax.rem(me + n - 2, n)
+        copies.append(
+            pltpu.make_async_copy(
+                (right, left)[d],
+                y.at[pl.ds(pl.multiple_of(d * half + b * rb, rb), rb), :],
+                sem.at[d],
+            )
+        )
+    for copy in copies:
+        copy.start()
+    for copy in copies:
+        copy.wait()
 
 
 def solution(mesh):
@@ -207,12 +279,15 @@
         rb = rows // 2 // n
         nj, nc = hidden // FB, cols // DB
         dma = pltpu.SemaphoreType.DMA
-        return pl.pallas_call(
+        bf16 = jnp.bfloat16
+        vmem, anywhere = pl.BlockSpec(memory_space=pltpu.VMEM), pl.BlockSpec(memory_space=pl.ANY)
+        whole = jax.ShapeDtypeStruct((rows, cols), bf16)
+        ring, right, left = pl.pallas_call(
             functools.partial(ring_kernel, n),
             name="mlp_ring",
-            out_shape=jax.ShapeDtypeStruct((rows, cols), jnp.bfloat16),
-            in_specs=[pl.BlockSpec(memory_space=pl.ANY)] * 4,
-            out_specs=pl.BlockSpec(memory_space=pl.ANY),
+            out_shape=(whole, pltpu.VMEM((rb, cols), bf16), pltpu.VMEM((rb, cols), bf16)),
+            in_specs=[anywhere] * 4,
+            out_specs=(anywhere, vmem, vmem),
             scratch_shapes=[
                 pltpu.VMEM(w_gate.shape, jnp.bfloat16),
                 pltpu.VMEM(w_up.shape, jnp.bfloat16),
@@ -232,9 +307,33 @@
                 dma((2, nc)),
             ],
             compiler_params=pltpu.CompilerParams(
-                collective_id=0, has_side_effects=True, vmem_limit_bytes=67043328
+                collective_id=0, has_side_effects=True, vmem_limit_bytes=61 * 2**20 + 2**19
             ),
         )(x, w_gate, w_up, w_down)
+        on_right = lax.ppermute(right, "tp", [(i, (i + 1) % n) for i in range(n)])
+        on_left = lax.ppermute(left, "tp", [(i, (i + n - 1) % n) for i in range(n)])
+        y = pl.pallas_call(
+            functools.partial(place_kernel, n),
+            name="place",
+            out_shape=whole,
+            in_specs=[anywhere, vmem, vmem],
+            out_specs=anywhere,
+            scratch_shapes=[pltpu.VMEM((2, n - 2, rb, cols), bf16), dma((2, n - 2)), dma((2, n - 1))],
+            compiler_params=pltpu.CompilerParams(vmem_limit_bytes=50 * 2**20),
+            cost_estimate=pl.CostEstimate(
+                flops=0, bytes_accessed=4 * rows * cols, transcendentals=0
+            ),
+        )(ring, right, left)
+        return pl.pallas_call(
+            functools.partial(place_last_kernel, n),
+            name="place_last",
+            out_shape=whole,
+            in_specs=[anywhere, vmem, vmem],
+            out_specs=anywhere,
+            input_output_aliases={0: 0},
+            scratch_shapes=[dma((2,))],
+            compiler_params=pltpu.CompilerParams(vmem_limit_bytes=50 * 2**20),
+        )(y, on_right, on_left)
 
     return jax.shard_map(
         step,

time: 356 us -> 344 us (0.966)
  local copies, waits for them, and re-layouts: 14.1 us -> 0 us
  Pallas kernels: 341 us -> 328 us
  waiting for transfers between devices: 0 us -> 12.1 us
    pallas_call x1, Pallas kernels: 341 us -> 317 us  [step(): pl.pallas_call(functools.partial(ring_kernel, n), name='mlp_ring', out_sh...]
    unnamed x1 -> x0, local copies, waits for them, and re-layouts: 14.1 us -> none
    ppermute x0 -> x2, waiting for transfers between devices: none -> 12.1 us  [the longest x1 12.1 us: step(): on_right = lax.ppermute(right, 'tp', [(i, (i + 1) % n) for i in range(n)])]
    pallas_call x0 -> x2, Pallas kernels: none -> 11.3 us  [the longest x1 10 us: step(): pl.pallas_call(functools.partial(place_kernel, n), name='place', out_shap...]
  transfers between devices with their start and end apart: 0 -> 2, of which waited for: 0 -> 1; matrix products, arithmetic and copies ran while one was open for 0% -> 0% of each run, Pallas kernels for 0% -> 3%
where the time goes in v3:
time: 344 us; the launch traced here: 343 us
  Pallas kernels  328 us (95%)
  waiting for transfers between devices  12.1 us (4%)
    pallas_call x1, Pallas kernels, step(): pl.pallas_call(functools.partial(ring_kernel, n), name='mlp_ring', out_sh...  317 us
    ppermute x1, waiting for transfers between devices, step(): on_right = lax.ppermute(right, 'tp', [(i, (i + 1) % n) for i in range(n)])  12.1 us
    pallas_call x1, Pallas kernels, step(): pl.pallas_call(functools.partial(place_kernel, n), name='place', out_shap...  10 us
  transfers between devices with their start and end apart: 2, of which 1 were waited for; matrix products, arithmetic and copies ran while one was open for 0% of the time, Pallas kernels for 3%

profile of v3, /device:TPU:21, one launch (start us, length us, event | category | flops | bytes accessed | tf_op | source)
XLA Modules:
  0.0 343.3 jit_solution(12997624977971661297)
XLA Ops:
  0.0 317.1 %mlp_ring.1 = (bf16[2048,4096]{1,0:T(8,128)(2,1)}, bf16[128,4096]{1,0:T(8,128)(2,1)S(1)}, bf16[128,4096]{1,0:T(8,128)(2,1)S(1)}) custom-call(bf16[2048,4096]{1,0:T(8,128)(2,1)} %x.1, bf16[4096,2048]{1,0:T(8,128)(2,1)} %wg.1, bf16[4096,2048]{1,0:T(8,128)(2,1)} %wu.1, bf16[2048,4096]{1,0:T(8,128)(2,1)} %wd.1), custom_call_target="tpu_custom_call" | custom-call | tf_op jit(solution)/shard_map/mlp_ring/pallas_call | solution.py:285
  317.1 0.1 collective-permute-start
  317.3 2.6 collective-permute-start.1
  319.9 10.0 %place.1._ = bf16[2048,4096]{1,0:T(8,128)(2,1)} custom-call(bf16[2048,4096]{1,0:T(8,128)(2,1)} %get-tuple-element.8.ring, bf16[128,4096]{1,0:T(8,128)(2,1)S(1)} %get-tuple-element.9.right, bf16[128,4096]{1,0:T(8,128)(2,1)S(1)} %get-tuple-element.10.left), custom_call_target="tpu_custom_call" | custom-call | bytes 33554432 | tf_op jit(solution)/shard_map/place/pallas_call | solution.py:315
  329.9 12.1 %collective-permute-done.right = bf16[128,4096]{1,0:T(8,128)(2,1)S(1)} collective-permute-done((bf16[128,4096]{1,0:T(8,128)(2,1)S(1)}, bf16[128,4096]{1,0:T(8,128)(2,1)S(1)}, u32[]{:S(2)}, u32[]{:S(2)}) %collective-permute-start) | collective-permute-done | bytes 1048608 | tf_op jit(solution)/shard_map/ppermute | solution.py:313
  342.0 0.0 collective-permute-done.1.left
  342.0 1.3 place_last.1
Async XLA Ops:
  317.1 24.8 %collective-permute-start = (bf16[128,4096]{1,0:T(8,128)(2,1)S(1)}, bf16[128,4096]{1,0:T(8,128)(2,1)S(1)}, u32[]{:S(2)}, u32[]{:S(2)}) collective-permute-start(bf16[128,4096]{1,0:T(8,128)(2,1)S(1)} %get-tuple-element.9.right), channel_id=1, source_target_pairs={{0,1},{1,2},{2,3},{3,4},{4,5},{5,6},{6,7},{7,0},{8,9},{9,10},{10,1... | collective-permute-start | bytes 3145736 | tf_op jit(solution)/shard_map/ppermute | solution.py:313
  317.3 24.7 %collective-permute-start.1 = (bf16[128,4096]{1,0:T(8,128)(2,1)S(1)}, bf16[128,4096]{1,0:T(8,128)(2,1)S(1)}, u32[]{:S(2)}, u32[]{:S(2)}) collective-permute-start(bf16[128,4096]{1,0:T(8,128)(2,1)S(1)} %get-tuple-element.10.left), channel_id=1, source_target_pairs={{0,7},{1,0},{2,1},{3,2},{4,3},{5,4},{6,5},{7,6},{8,15},{9,8},{10,9... | collective-permute-start | bytes 3145736 | tf_op jit(solution)/shard_map/ppermute | solution.py:314

commit v4 on v3

--- a/solution.py
+++ b/solution.py
@@ -85,9 +85,8 @@
 
     for d in range(2):
         load_x(d, 0).start()
-    for j in range(2):
-        for copy in load_w(j):
-            copy.start()
+    for copy in load_w(0):
+        copy.start()
 
     barrier = pltpu.get_barrier_semaphore()
     for peer in peers:
@@ -97,6 +96,11 @@
     def ring_step(s, _):
         for d in range(2):
             load_x(d, s).wait()
+
+        @pl.when(s == 0)
+        def _():
+            for copy in load_w(1):
+                copy.start()
 
         def gate_up(j, _):
             @pl.when(s == 0)

time: 344 us -> 344 us (level)
  no operation moved by 1% of the time
where the time goes in v4:
time: 344 us; the launch traced here: 343 us
  Pallas kernels  328 us (95%)
  waiting for transfers between devices  12.1 us (4%)
    pallas_call x1, Pallas kernels, step(): pl.pallas_call(functools.partial(ring_kernel, n), name='mlp_ring', out_sh...  317 us
    ppermute x1, waiting for transfers between devices, step(): on_right = lax.ppermute(right, 'tp', [(i, (i + 1) % n) for i in range(n)])  12.1 us
    pallas_call x1, Pallas kernels, step(): pl.pallas_call(functools.partial(place_kernel, n), name='place', out_shap...  10 us
  transfers between devices with their start and end apart: 2, of which 1 were waited for; matrix products, arithmetic and copies ran while one was open for 0% of the time, Pallas kernels for 3%

profile of v4, /device:TPU:21, one launch (start us, length us, event | category | flops | bytes accessed | tf_op | source)
XLA Modules:
  0.0 343.2 jit_solution(16940683276867282091)
XLA Ops:
  0.0 317.0 %mlp_ring.1 = (bf16[2048,4096]{1,0:T(8,128)(2,1)}, bf16[128,4096]{1,0:T(8,128)(2,1)S(1)}, bf16[128,4096]{1,0:T(8,128)(2,1)S(1)}) custom-call(bf16[2048,4096]{1,0:T(8,128)(2,1)} %x.1, bf16[4096,2048]{1,0:T(8,128)(2,1)} %wg.1, bf16[4096,2048]{1,0:T(8,128)(2,1)} %wu.1, bf16[2048,4096]{1,0:T(8,128)(2,1)} %wd.1), custom_call_target="tpu_custom_call" | custom-call | tf_op jit(solution)/shard_map/mlp_ring/pallas_call | solution.py:289
  317.0 0.1 collective-permute-start
  317.1 2.6 collective-permute-start.1
  319.8 10.0 %place.1._ = bf16[2048,4096]{1,0:T(8,128)(2,1)} custom-call(bf16[2048,4096]{1,0:T(8,128)(2,1)} %get-tuple-element.8.ring, bf16[128,4096]{1,0:T(8,128)(2,1)S(1)} %get-tuple-element.9.right, bf16[128,4096]{1,0:T(8,128)(2,1)S(1)} %get-tuple-element.10.left), custom_call_target="tpu_custom_call" | custom-call | bytes 33554432 | tf_op jit(solution)/shard_map/place/pallas_call | solution.py:319
  329.8 12.1 %collective-permute-done.right = bf16[128,4096]{1,0:T(8,128)(2,1)S(1)} collective-permute-done((bf16[128,4096]{1,0:T(8,128)(2,1)S(1)}, bf16[128,4096]{1,0:T(8,128)(2,1)S(1)}, u32[]{:S(2)}, u32[]{:S(2)}) %collective-permute-start) | collective-permute-done | bytes 1048608 | tf_op jit(solution)/shard_map/ppermute | solution.py:317
  341.8 0.0 collective-permute-done.1.left
  341.9 1.3 place_last.1
Async XLA Ops:
  317.0 24.8 %collective-permute-start = (bf16[128,4096]{1,0:T(8,128)(2,1)S(1)}, bf16[128,4096]{1,0:T(8,128)(2,1)S(1)}, u32[]{:S(2)}, u32[]{:S(2)}) collective-permute-start(bf16[128,4096]{1,0:T(8,128)(2,1)S(1)} %get-tuple-element.9.right), channel_id=1, source_target_pairs={{0,1},{1,2},{2,3},{3,4},{4,5},{5,6},{6,7},{7,0},{8,9},{9,10},{10,1... | collective-permute-start | bytes 3145736 | tf_op jit(solution)/shard_map/ppermute | solution.py:317
  317.1 24.7 %collective-permute-start.1 = (bf16[128,4096]{1,0:T(8,128)(2,1)S(1)}, bf16[128,4096]{1,0:T(8,128)(2,1)S(1)}, u32[]{:S(2)}, u32[]{:S(2)}) collective-permute-start(bf16[128,4096]{1,0:T(8,128)(2,1)S(1)} %get-tuple-element.10.left), channel_id=1, source_target_pairs={{0,7},{1,0},{2,1},{3,2},{4,3},{5,4},{6,5},{7,6},{8,15},{9,8},{10,9... | collective-permute-start | bytes 3145736 | tf_op jit(solution)/shard_map/ppermute | solution.py:318
